TPU v7x, 256 devices: a whole 4x4x8 slice. The times are simulated.
256 devices in a mesh: row: 8 (over y, core), col: 32 (over z, x).
Axes of the slice: x: 4, y: 4, z: 8, core: 2. Of those that a mesh axis runs over, the one named last changes fastest.
Arguments:
- rhs: bfloat16 [6144, 6144], P('row', 'col'), may hold values from -6 to 6
- basis_left: bfloat16 [6144, 6144], P('col', 'row'), may hold values from -1 to 1, as said below
- basis_right: bfloat16 [6144, 6144], P('row', 'col'), may hold values from -1 to 1, as said below
- eig_left: float32 [6144], P('row'), may hold values from 0.1 to 4
- eig_right: float32 [6144], P('col'), may hold values from 0.1 to 4
Outputs:
- solution: bfloat16 [6144, 6144], P('col', 'row')
Inputs may be any that keep to these rules, and one draw needn't show every extreme that they name: `basis_left`: an orthogonal matrix drawn uniformly, rounded to bfloat16. `basis_right`: an orthogonal matrix drawn uniformly, rounded to bfloat16.
All inputs are finite; a program needn't handle non-finite values.
Results may differ from a plain program's by a relative error of at most 0.0085.
Values may be sent and summed in bfloat16 or wider, within the bound.
No kernel may reach another device: no remote copies, remote signals or barrier semaphores. Data moves between devices by JAX's collectives and lax.ppermute only.
A program may use at most 64 MiB of HBM per device.

v0:
```python
import jax
import jax.numpy as jnp
from jax import lax
from jax.sharding import Mesh, PartitionSpec as P

F32, BF16 = (jnp.float32, jnp.bfloat16)
ROW = ("y", "core")


def dot(a, b, over):
    return lax.dot_general(a, b, ((over[:1], over[1:]), ((), ())), preferred_element_type=F32)


def gathered(shard, axis, dim):
    copies = jnp.broadcast_to(shard, (lax.axis_size(axis), *shard.shape))
    parts = lax.all_to_all(copies, axis, 0, 0, tiled=True)
    if dim == 0:
        return parts.reshape(-1, parts.shape[-1])
    return jnp.moveaxis(parts, 0, 1).reshape(parts.shape[1], -1)


def summed(partial, axis):
    peers = lax.axis_size(axis)
    parts = partial.reshape(peers, partial.shape[0] // peers, partial.shape[1])
    parts = lax.all_to_all(parts, axis, 0, 0, tiled=True)
    return jnp.sum(parts.astype(F32), axis=0)


def body(rhs, basis_left, basis_right, eig_left, eig_right):
    row_of = [(z * 8 + r, r * 8 + z) for z in range(8) for r in range(8)]
    left = lax.all_gather(basis_left, "z", axis=0, tiled=True)
    c_part = lax.all_to_all(rhs, "x", 0, 1, tiled=True)
    c_block = gathered(c_part, ROW, 0)
    turned = lax.ppermute(basis_right, (*ROW, "z"), row_of)
    right = lax.all_gather(turned, ROW, axis=1, tiled=True)
    part = dot(left, c_block, (0, 0)).astype(BF16)
    projected = gathered(summed(part, "x").astype(BF16), "x", 0)
    part = dot(projected, right, (1, 0)).astype(BF16)
    second = lax.psum_scatter(part, "z", scatter_dimension=1, tiled=True).astype(F32)
    scaled = (second / (eig_left[:, None] + eig_right[None, :])).astype(BF16)
    basis_right, _ = lax.optimization_barrier((basis_right, part))
    right = lax.all_gather(basis_right, "x", axis=1, tiled=True)
    scaled = gathered(scaled, "x", 1)
    part = dot(left, scaled, (1, 0)).astype(BF16)
    half = summed(part, "core").astype(BF16)
    half = summed(half, "y").astype(BF16)
    half = gathered(gathered(half, "y", 0), "core", 0)
    part = dot(half, right, (1, 1)).astype(BF16)
    return lax.psum_scatter(part, "z", scatter_dimension=0, tiled=True)


def solution(mesh):
    split = Mesh(mesh.devices.reshape(4, 2, 8, 4), ("y", "core", "z", "x"))
    row, col = (ROW, ("z", "x"))
    in_specs = (P(row, col), P(col, row), P(row, col), P(row), P(col))
    return jax.shard_map(
        body, mesh=split, in_specs=in_specs, out_specs=P(col, row), check_vma=False
    )
```

profile of v0, /device:TPU:14, one launch (start us, length us, event | category | flops | bytes accessed | tf_op | source)
XLA Modules:
  0.0 283.0 jit_solution(11018644528555109359)
XLA Ops:
  7.3 1.9 copy.19
  9.1 4.8 %all-to-all-start = ((bf16[4,192,192]{2,1,0:T(8,128)(2,1)}), bf16[4,192,192]{2,1,0:T(8,128)(2,1)S(1)}, u32[]{:S(2)}, u32[]{:S(2)}) async-start(bf16[4,192,192]{2,1,0:T(8,128)(2,1)} %bitcast), calls=%async_computation | async-start | bytes 786432 | tf_op jit(solution)/shard_map/all_to_all | solution.py:32
  13.9 5.1 %collective-permute-start = (bf16[768,192]{0,1:T(8,128)(2,1)}, bf16[768,192]{0,1:T(8,128)(2,1)S(1)}, u32[]{:S(2)}, u32[]{:S(2)}) collective-permute-start(bf16[768,192]{0,1:T(8,128)(2,1)} %param.7), channel_id=1, source_target_pairs={{0,0},{4,32},{8,64},{12,96},{16,128},{20,160},{24,192},{28,224},{3... | collective-permute-start | bytes 884744 | tf_op jit(solution)/shard_map/ppermute | solution.py:34
  19.0 0.9 all-to-all-done
  20.6 1.6 broadcast_in_dim.17
  22.2 7.8 %all-to-all-start.1 = ((bf16[8,192,768]{2,1,0:T(8,128)(2,1)}), bf16[8,192,768]{2,1,0:T(8,128)(2,1)S(1)}, u32[]{:S(2)}, u32[]{:S(2)}) async-start(bf16[8,192,768]{2,1,0:T(8,128)(2,1)} %broadcast_in_dim.17), calls=%async_computation.1 | async-start | bytes 4718592 | tf_op jit(solution)/shard_map/all_to_all | solution.py:16
  30.0 16.2 %collective-permute-done = bf16[768,192]{0,1:T(8,128)(2,1)S(1)} collective-permute-done((bf16[768,192]{0,1:T(8,128)(2,1)}, bf16[768,192]{0,1:T(8,128)(2,1)S(1)}, u32[]{:S(2)}, u32[]{:S(2)}) %collective-permute-start) | collective-permute-done | bytes 294944 | tf_op jit(solution)/shard_map/ppermute | solution.py:34
  47.0 11.5 %all-to-all-done.1 = bf16[8,192,768]{2,1,0:T(8,128)(2,1)S(1)} async-done(((bf16[8,192,768]{2,1,0:T(8,128)(2,1)}), bf16[8,192,768]{2,1,0:T(8,128)(2,1)S(1)}, u32[]{:S(2)}, u32[]{:S(2)}) %all-to-all-start.1) | async-done | bytes 2359328 | tf_op jit(solution)/shard_map/all_to_all | solution.py:16
  58.5 8.3 %all-gather.4.cloned.1.call-done = bf16[1536,768]{1,0:T(8,128)(2,1)} async-done(((bf16[192,768]{1,0:T(8,128)(2,1)}), bf16[1536,768]{1,0:T(8,128)(2,1)}) %all-gather.4.cloned.1.call-update) | async-done | bytes 2359312 | tf_op jit(solution)/shard_map/all_gather | solution.py:31
  66.8 3.7 %convolution_convert_fusion.3 = bf16[768,768]{1,0:T(8,128)(2,1)S(1)} fusion(bf16[1536,768]{1,0:T(8,128)(2,1)} %all-gather.4.cloned.1.call-done, bf16[1536,768]{1,0:T(8,128)(2,1)S(1)} %bitcast.30), kind=kOutput, calls=%fused_computation.4 | convolution fusion | flops 1812529152 | bytes 5898240 | tf_op jit(solution)/shard_map/dot_general | solution.py:11
  70.5 16.7 %all_to_all.59 = bf16[4,192,768]{2,1,0:T(8,128)(2,1)S(1)} all-to-all(bf16[4,192,768]{2,1,0:T(8,128)(2,1)S(1)} %bitcast.36), channel_id=1, replica_groups=mesh['y'=4,'core'=2,'z'=8,'x'=4] {'x'}, dimensions={0} | all-to-all | bytes 2359296 | tf_op jit(solution)/shard_map/all_to_all | solution.py:25
  87.5 1.1 broadcast_in_dim.18
  88.6 5.6 %all-to-all-start.3 = ((bf16[4,192,768]{2,1,0:T(8,128)(2,1)}), bf16[4,192,768]{2,1,0:T(8,128)(2,1)S(1)}, u32[]{:S(2)}, u32[]{:S(2)}) async-start(bf16[4,192,768]{2,1,0:T(8,128)(2,1)} %broadcast_in_dim.18), calls=%async_computation.3 | async-start | bytes 2359296 | tf_op jit(solution)/shard_map/all_to_all | solution.py:16
  94.1 1.1 all-gather.6.cloned.1.call-done
  95.2 10.2 %all-to-all-done.3 = bf16[4,192,768]{2,1,0:T(8,128)(2,1)S(1)} async-done(((bf16[4,192,768]{2,1,0:T(8,128)(2,1)}), bf16[4,192,768]{2,1,0:T(8,128)(2,1)S(1)}, u32[]{:S(2)}, u32[]{:S(2)}) %all-to-all-start.3) | async-done | bytes 1179680 | tf_op jit(solution)/shard_map/all_to_all | solution.py:16
  105.4 3.7 %convolution_convert_fusion.2 = bf16[768,1536]{1,0:T(8,128)(2,1)S(1)} fusion(bf16[768,768]{1,0:T(8,128)(2,1)S(1)} %bitcast.34, bf16[768,1536]{0,1:T(8,128)(2,1)} %all-gather.6.cloned.1.call-done), kind=kOutput, calls=%fused_computation.2 | convolution fusion | flops 1813118976 | bytes 5898240 | tf_op jit(solution)/shard_map/dot_general | solution.py:11
  109.1 2.5 copy.25
  111.6 44.1 %reduce-scatter.7.cloned.1.call-done = bf16[192,768]{1,0:T(8,128)(2,1)} async-done(((bf16[1536,768]{1,0:T(8,128)(2,1)}), bf16[192,768]{1,0:T(8,128)(2,1)}) %reduce-scatter.7.cloned.1.call-update) | async-done | bytes 294928
  155.7 1.1 divide_convert_fusion
  156.9 14.7 %all_to_all.60 = bf16[4,768,192]{1,2,0:T(8,128)(2,1)S(1)} all-to-all(bf16[4,768,192]{1,2,0:T(8,128)(2,1)S(1)} %broadcast_in_dim.19), channel_id=1, replica_groups=mesh['y'=4,'core'=2,'z'=8,'x'=4] {'x'}, dimensions={0} | all-to-all | bytes 2359296 | tf_op jit(solution)/shard_map/all_to_all | solution.py:16
  171.6 2.0 convolution_convert_fusion.1
  173.8 5.6 %all_to_all.61 = bf16[2,768,768]{1,2,0:T(8,128)(2,1)S(1)} all-to-all(bf16[2,768,768]{1,2,0:T(8,128)(2,1)S(1)} %bitcast.28), channel_id=1, replica_groups=mesh['y'=4,'core'=2,'z'=8,'x'=4] {'core'}, dimensions={0} | all-to-all | bytes 4718592 | tf_op jit(solution)/shard_map/all_to_all | solution.py:25
  179.4 1.2 reduce_sum.37
  180.6 1.4 copy.24
  182.1 4.8 %all-to-all-start.6 = ((bf16[4,192,768]{2,1,0:T(8,128)(2,1)}), bf16[4,192,768]{2,1,0:T(8,128)(2,1)S(1)}, u32[]{:S(2)}, u32[]{:S(2)}) async-start(bf16[4,192,768]{2,1,0:T(8,128)(2,1)} %bitcast.8), calls=%async_computation.6 | async-start | bytes 2359296 | tf_op jit(solution)/shard_map/all_to_all | solution.py:25
  187.4 14.8 %all-to-all-done.6 = bf16[4,192,768]{2,1,0:T(8,128)(2,1)S(1)} async-done(((bf16[4,192,768]{2,1,0:T(8,128)(2,1)}), bf16[4,192,768]{2,1,0:T(8,128)(2,1)S(1)}, u32[]{:S(2)}, u32[]{:S(2)}) %all-to-all-start.6) | async-done | bytes 1179680 | tf_op jit(solution)/shard_map/all_to_all | solution.py:25
  202.6 18.4 %all_to_all.62 = bf16[4,192,768]{2,1,0:T(8,128)(2,1)S(1)} all-to-all(bf16[4,192,768]{2,1,0:T(8,128)(2,1)S(1)} %broadcast_in_dim.20), channel_id=1, replica_groups=mesh['y'=4,'core'=2,'z'=8,'x'=4] {'y'}, dimensions={0} | all-to-all | bytes 2359296 | tf_op jit(solution)/shard_map/all_to_all | solution.py:16
  220.9 1.6 broadcast_in_dim.21
  222.5 3.8 %all-to-all-start.8 = ((bf16[2,768,768]{2,1,0:T(8,128)(2,1)}), bf16[2,768,768]{2,1,0:T(8,128)(2,1)S(1)}, u32[]{:S(2)}, u32[]{:S(2)}) async-start(bf16[2,768,768]{2,1,0:T(8,128)(2,1)} %broadcast_in_dim.21), calls=%async_computation.8 | async-start | bytes 4718592 | tf_op jit(solution)/shard_map/all_to_all | solution.py:16
  226.4 3.0 %all-to-all-done.8 = bf16[2,768,768]{2,1,0:T(8,128)(2,1)S(1)} async-done(((bf16[2,768,768]{2,1,0:T(8,128)(2,1)}), bf16[2,768,768]{2,1,0:T(8,128)(2,1)S(1)}, u32[]{:S(2)}, u32[]{:S(2)}) %all-to-all-start.8) | async-done | bytes 2359328 | tf_op jit(solution)/shard_map/all_to_all | solution.py:16
  229.4 4.7 %convolution_convert_fusion = bf16[1536,768]{1,0:T(8,128)(2,1)} fusion(bf16[1536,768]{1,0:T(8,128)(2,1)S(1)} %bitcast.31, bf16[768,768]{0,1:T(8,128)(2,1)} %all-gather.8.cloned.1.call-done), kind=kOutput, calls=%fused_computation | convolution fusion | flops 1813118976 | bytes 5898240 | tf_op jit(solution)/shard_map/dot_general | solution.py:11
  234.1 42.3 %reduce-scatter.5.cloned.1.call-done = bf16[192,768]{1,0:T(8,128)(2,1)} async-done(((bf16[1536,768]{1,0:T(8,128)(2,1)}), bf16[192,768]{1,0:T(8,128)(2,1)}) %reduce-scatter.5.cloned.1.call-update) | async-done | bytes 294928 | tf_op jit(solution)/shard_map/reduce_scatter | solution.py:49
  (26 shorter events, 3.6 us)
Async XLA Ops:
  6.5 60.2 %all-gather.4.cloned.1.call-start = ((), (), s32[]{:S(2)}) async-start(), calls=%async_computation.11 | async-start | bytes 2654208 | tf_op jit(solution)/shard_map/all_gather | solution.py:31
  9.1 10.8 %all-to-all-start = ((bf16[4,192,192]{2,1,0:T(8,128)(2,1)}), bf16[4,192,192]{2,1,0:T(8,128)(2,1)S(1)}, u32[]{:S(2)}, u32[]{:S(2)}) async-start(bf16[4,192,192]{2,1,0:T(8,128)(2,1)} %bitcast), calls=%async_computation | async-start | bytes 786432 | tf_op jit(solution)/shard_map/all_to_all | solution.py:32
  13.9 32.3 %collective-permute-start = (bf16[768,192]{0,1:T(8,128)(2,1)}, bf16[768,192]{0,1:T(8,128)(2,1)S(1)}, u32[]{:S(2)}, u32[]{:S(2)}) collective-permute-start(bf16[768,192]{0,1:T(8,128)(2,1)} %param.7), channel_id=1, source_target_pairs={{0,0},{4,32},{8,64},{12,96},{16,128},{20,160},{24,192},{28,224},{3... | collective-permute-start | bytes 884744 | tf_op jit(solution)/shard_map/ppermute | solution.py:34
  22.2 36.3 %all-to-all-start.1 = ((bf16[8,192,768]{2,1,0:T(8,128)(2,1)}), bf16[8,192,768]{2,1,0:T(8,128)(2,1)S(1)}, u32[]{:S(2)}, u32[]{:S(2)}) async-start(bf16[8,192,768]{2,1,0:T(8,128)(2,1)} %broadcast_in_dim.17), calls=%async_computation.1 | async-start | bytes 4718592 | tf_op jit(solution)/shard_map/all_to_all | solution.py:16
  30.0 65.2 %all-gather.6.cloned.1.call-start = ((), (), s32[]{:S(2)}) async-start(), calls=%async_computation.12 | async-start | bytes 2654208 | tf_op jit(solution)/shard_map/all_gather | solution.py:35
  46.2 0.7 copy-start
  88.6 16.8 %all-to-all-start.3 = ((bf16[4,192,768]{2,1,0:T(8,128)(2,1)}), bf16[4,192,768]{2,1,0:T(8,128)(2,1)S(1)}, u32[]{:S(2)}, u32[]{:S(2)}) async-start(bf16[4,192,768]{2,1,0:T(8,128)(2,1)} %broadcast_in_dim.18), calls=%async_computation.3 | async-start | bytes 2359296 | tf_op jit(solution)/shard_map/all_to_all | solution.py:16
  94.1 61.6 %reduce-scatter.7.cloned.1.call-start = ((), (), s32[]{:S(2)}) async-start(), calls=%async_computation.15 | async-start | bytes 2654208
  111.5 44.2 %copy-start.1 = (f32[768]{0:T(1024)S(1)}, f32[768]{0:T(1024)}, u32[]{:S(2)}) copy-start(f32[768]{0:T(1024)} %param.8) | copy-start | bytes 9220
  111.5 44.2 %copy-start.2 = (f32[192]{0:T(256)S(1)}, f32[192]{0:T(256)}, u32[]{:S(2)}) copy-start(f32[192]{0:T(256)} %param.9) | copy-start | bytes 2308
  111.6 60.0 %copy-start.3 = (bf16[1536,768]{1,0:T(8,128)(2,1)S(1)}, bf16[1536,768]{1,0:T(8,128)(2,1)}, u32[]{:S(2)}) copy-start(bf16[1536,768]{1,0:T(8,128)(2,1)} %all-gather.4.cloned.1.call-done) | copy-start | bytes 7077892
  182.1 20.1 %all-to-all-start.6 = ((bf16[4,192,768]{2,1,0:T(8,128)(2,1)}), bf16[4,192,768]{2,1,0:T(8,128)(2,1)S(1)}, u32[]{:S(2)}, u32[]{:S(2)}) async-start(bf16[4,192,768]{2,1,0:T(8,128)(2,1)} %bitcast.8), calls=%async_computation.6 | async-start | bytes 2359296 | tf_op jit(solution)/shard_map/all_to_all | solution.py:25
  186.9 39.5 %all-gather.8.cloned.1.call-start = ((), (), s32[]{:S(2)}) async-start(), calls=%async_computation.13 | async-start | bytes 1474560 | tf_op jit(solution)/shard_map/all_gather | solution.py:42
  222.5 6.9 %all-to-all-start.8 = ((bf16[2,768,768]{2,1,0:T(8,128)(2,1)}), bf16[2,768,768]{2,1,0:T(8,128)(2,1)S(1)}, u32[]{:S(2)}, u32[]{:S(2)}) async-start(bf16[2,768,768]{2,1,0:T(8,128)(2,1)} %broadcast_in_dim.21), calls=%async_computation.8 | async-start | bytes 4718592 | tf_op jit(solution)/shard_map/all_to_all | solution.py:16
  226.3 50.1 %reduce-scatter.5.cloned.1.call-start = ((), (), s32[]{:S(2)}) async-start(), calls=%async_computation.14 | async-start | bytes 2654208 | tf_op jit(solution)/shard_map/reduce_scatter | solution.py:49
Sparse Core Ops, SparseCore 0:
  9.1 57.5 all-gather.3
  68.6 26.5 all-gather.5
  111.7 43.9 reduce-scatter.6
  189.2 25.5 all-gather.7
  234.2 42.1 reduce-scatter.4
where the time goes:
time: 284 us; the launch traced here: 283 us
  waiting for transfers between devices  154 us (54%)
  blocking collectives  55.4 us (20%)
  starting transfers between devices  31.8 us (11%)
  matrix products  14.1 us (5%)
  between operations  13.2 us (5%)
  local copies, waits for them, and re-layouts  11.8 us (4%)
  other arithmetic  2.88 us (1%)
    unnamed x6, waiting for transfers between devices  45.4 us
    reduce_scatter x1, waiting for transfers between devices, body(): return lax.psum_scatter(part, 'z', scatter_dimension=0, tiled=True)  42.3 us
    all_to_all x2, blocking collectives, gathered(): parts = lax.all_to_all(copies, axis, 0, 0, tiled=True)  33.1 us
    all_to_all x3, waiting for transfers between devices, gathered(): parts = lax.all_to_all(copies, axis, 0, 0, tiled=True)  24.7 us
    all_to_all x2, blocking collectives, summed(): parts = lax.all_to_all(parts, axis, 0, 0, tiled=True)  22.3 us
    all_to_all x3, starting transfers between devices, gathered(): parts = lax.all_to_all(copies, axis, 0, 0, tiled=True)  17.2 us
    ppermute x1, waiting for transfers between devices, body(): turned = lax.ppermute(basis_right, (*ROW, 'z'), row_of)  16.2 us
    all_to_all x1, waiting for transfers between devices, summed(): parts = lax.all_to_all(parts, axis, 0, 0, tiled=True)  14.8 us
  transfers between devices with their start and end apart: 11, of which 10 were waited for; matrix products, arithmetic and copies ran while one was open for 4% of the time, Pallas kernels for 0%

commit v1 on v0

--- a/solution.py
+++ b/solution.py
@@ -29,7 +29,9 @@
 def body(rhs, basis_left, basis_right, eig_left, eig_right):
     row_of = [(z * 8 + r, r * 8 + z) for z in range(8) for r in range(8)]
     left = lax.all_gather(basis_left, "z", axis=0, tiled=True)
-    c_part = lax.all_to_all(rhs, "x", 0, 1, tiled=True)
+    c_part = jnp.concatenate(
+        lax.all_to_all(jnp.stack(jnp.split(rhs, lax.axis_size("x"), axis=0)), "x", 0, 0), axis=1
+    )
     c_block = gathered(c_part, ROW, 0)
     turned = lax.ppermute(basis_right, (*ROW, "z"), row_of)
     right = lax.all_gather(turned, ROW, axis=1, tiled=True)

time: 284 us -> 283 us (level)
  no operation moved by 1% of the time
where the time goes in v1:
time: 283 us; the launch traced here: 282 us
  waiting for transfers between devices  153 us (54%)
  blocking collectives  55 us (19%)
  starting transfers between devices  32.2 us (11%)
  matrix products  14.1 us (5%)
  between operations  13.2 us (5%)
  local copies, waits for them, and re-layouts  10.6 us (4%)
  other arithmetic  3.72 us (1%)
    unnamed x6, waiting for transfers between devices  45.7 us
    reduce_scatter x1, waiting for transfers between devices, body(): return lax.psum_scatter(part, 'z', scatter_dimension=0, tiled=True)  41.1 us
    all_to_all x2, blocking collectives, gathered(): parts = lax.all_to_all(copies, axis, 0, 0, tiled=True)  32.6 us
    all_to_all x3, waiting for transfers between devices, gathered(): parts = lax.all_to_all(copies, axis, 0, 0, tiled=True)  24.4 us
    all_to_all x2, blocking collectives, summed(): parts = lax.all_to_all(parts, axis, 0, 0, tiled=True)  22.3 us
    all_to_all x3, starting transfers between devices, gathered(): parts = lax.all_to_all(copies, axis, 0, 0, tiled=True)  17.2 us
    ppermute x1, waiting for transfers between devices, body(): turned = lax.ppermute(basis_right, (*ROW, 'z'), row_of)  16.5 us
    all_to_all x1, waiting for transfers between devices, summed(): parts = lax.all_to_all(parts, axis, 0, 0, tiled=True)  14.8 us
  transfers between devices with their start and end apart: 11, of which 10 were waited for; matrix products, arithmetic and copies ran while one was open for 4% of the time, Pallas kernels for 0%

profile of v1, /device:TPU:14, one launch (start us, length us, event | category | flops | bytes accessed | tf_op | source)
XLA Modules:
  0.0 281.9 jit_solution(1134754273605732889)
XLA Ops:
  7.3 1.2 slice_bitcast_fusion.3
  9.3 4.8 %all-to-all-start = ((bf16[4,192,192]{1,2,0:T(8,128)(2,1)}), bf16[4,192,192]{1,2,0:T(8,128)(2,1)S(1)}, u32[]{:S(2)}, u32[]{:S(2)}) async-start(bf16[4,192,192]{1,2,0:T(8,128)(2,1)} %pad_maximum_fusion), calls=%async_computation | async-start | bytes 786432 | tf_op jit(solution)/shard_map/all_to_all | solution.py:33
  14.1 5.1 %collective-permute-start = (bf16[768,192]{0,1:T(8,128)(2,1)S(1)}, bf16[768,192]{0,1:T(8,128)(2,1)S(1)}, u32[]{:S(2)}, u32[]{:S(2)}) collective-permute-start(bf16[768,192]{0,1:T(8,128)(2,1)S(1)} %copy-done), channel_id=1, source_target_pairs={{0,0},{4,32},{8,64},{12,96},{16,128},{20,160},{24,192},{28,224},{3... | collective-permute-start | bytes 884744 | tf_op jit(solution)/shard_map/ppermute | solution.py:36
  19.1 0.9 all-to-all-done
  20.2 1.6 broadcast_in_dim.17
  21.8 7.8 %all-to-all-start.1 = ((bf16[8,192,768]{2,1,0:T(8,128)(2,1)}), bf16[8,192,768]{2,1,0:T(8,128)(2,1)S(1)}, u32[]{:S(2)}, u32[]{:S(2)}) async-start(bf16[8,192,768]{2,1,0:T(8,128)(2,1)} %broadcast_in_dim.17), calls=%async_computation.1 | async-start | bytes 4718592 | tf_op jit(solution)/shard_map/all_to_all | solution.py:16
  29.6 16.5 %collective-permute-done = bf16[768,192]{0,1:T(8,128)(2,1)S(1)} collective-permute-done((bf16[768,192]{0,1:T(8,128)(2,1)S(1)}, bf16[768,192]{0,1:T(8,128)(2,1)S(1)}, u32[]{:S(2)}, u32[]{:S(2)}) %collective-permute-start) | collective-permute-done | bytes 294944 | tf_op jit(solution)/shard_map/ppermute | solution.py:36
  46.9 11.2 %all-to-all-done.1 = bf16[8,192,768]{2,1,0:T(8,128)(2,1)S(1)} async-done(((bf16[8,192,768]{2,1,0:T(8,128)(2,1)}), bf16[8,192,768]{2,1,0:T(8,128)(2,1)S(1)}, u32[]{:S(2)}, u32[]{:S(2)}) %all-to-all-start.1) | async-done | bytes 2359328 | tf_op jit(solution)/shard_map/all_to_all | solution.py:16
  58.1 8.6 %all-gather.4.cloned.1.call-done = bf16[1536,768]{1,0:T(8,128)(2,1)} async-done(((bf16[192,768]{1,0:T(8,128)(2,1)}), bf16[1536,768]{1,0:T(8,128)(2,1)}) %all-gather.4.cloned.1.call-update) | async-done | bytes 2359312 | tf_op jit(solution)/shard_map/all_gather | solution.py:31
  66.7 3.7 %convolution_convert_fusion.3 = bf16[768,768]{0,1:T(8,128)(2,1)S(1)} fusion(bf16[1536,768]{1,0:T(8,128)(2,1)S(1)} %bitcast.41, bf16[1536,768]{1,0:T(8,128)(2,1)} %all-gather.4.cloned.1.call-done), kind=kOutput, calls=%fused_computation.4 | convolution fusion | flops 1812529152 | bytes 5898240 | tf_op jit(solution)/shard_map/dot_general | solution.py:11
  70.4 16.7 %all_to_all.45 = bf16[4,192,768]{2,1,0:T(8,128)(2,1)S(1)} all-to-all(bf16[4,192,768]{2,1,0:T(8,128)(2,1)S(1)} %bitcast.47), channel_id=1, replica_groups=mesh['y'=4,'core'=2,'z'=8,'x'=4] {'x'}, dimensions={0} | all-to-all | bytes 2359296 | tf_op jit(solution)/shard_map/all_to_all | solution.py:25
  87.4 1.1 broadcast_in_dim.18
  88.5 5.6 %all-to-all-start.3 = ((bf16[4,192,768]{2,1,0:T(8,128)(2,1)}), bf16[4,192,768]{2,1,0:T(8,128)(2,1)S(1)}, u32[]{:S(2)}, u32[]{:S(2)}) async-start(bf16[4,192,768]{2,1,0:T(8,128)(2,1)} %broadcast_in_dim.18), calls=%async_computation.3 | async-start | bytes 2359296 | tf_op jit(solution)/shard_map/all_to_all | solution.py:16
  94.1 1.1 all-gather.6.cloned.1.call-done
  95.2 10.2 %all-to-all-done.3 = bf16[4,192,768]{2,1,0:T(8,128)(2,1)S(1)} async-done(((bf16[4,192,768]{2,1,0:T(8,128)(2,1)}), bf16[4,192,768]{2,1,0:T(8,128)(2,1)S(1)}, u32[]{:S(2)}, u32[]{:S(2)}) %all-to-all-start.3) | async-done | bytes 1179680 | tf_op jit(solution)/shard_map/all_to_all | solution.py:16
  105.3 3.7 %convolution_convert_fusion.2 = bf16[768,1536]{1,0:T(8,128)(2,1)S(1)} fusion(bf16[768,768]{1,0:T(8,128)(2,1)S(1)} %bitcast.45, bf16[768,1536]{0,1:T(8,128)(2,1)} %all-gather.6.cloned.1.call-done), kind=kOutput, calls=%fused_computation.2 | convolution fusion | flops 1813118976 | bytes 5898240 | tf_op jit(solution)/shard_map/dot_general | solution.py:11
  109.0 2.4 copy.23
  111.5 44.4 %reduce-scatter.7.cloned.1.call-done = bf16[192,768]{1,0:T(8,128)(2,1)} async-done(((bf16[1536,768]{1,0:T(8,128)(2,1)}), bf16[192,768]{1,0:T(8,128)(2,1)}) %reduce-scatter.7.cloned.1.call-update) | async-done | bytes 294928
  155.9 1.1 divide_convert_fusion
  157.1 14.3 %all_to_all.46 = bf16[4,768,192]{1,2,0:T(8,128)(2,1)S(1)} all-to-all(bf16[4,768,192]{1,2,0:T(8,128)(2,1)S(1)} %broadcast_in_dim.19), channel_id=1, replica_groups=mesh['y'=4,'core'=2,'z'=8,'x'=4] {'x'}, dimensions={0} | all-to-all | bytes 2359296 | tf_op jit(solution)/shard_map/all_to_all | solution.py:16
  171.4 2.0 convolution_convert_fusion.1
  173.6 5.6 %all_to_all.47 = bf16[2,768,768]{1,2,0:T(8,128)(2,1)S(1)} all-to-all(bf16[2,768,768]{1,2,0:T(8,128)(2,1)S(1)} %bitcast.39), channel_id=1, replica_groups=mesh['y'=4,'core'=2,'z'=8,'x'=4] {'core'}, dimensions={0} | all-to-all | bytes 4718592 | tf_op jit(solution)/shard_map/all_to_all | solution.py:25
  179.2 1.2 reduce_sum.37
  180.4 1.5 copy.22
  181.9 5.2 %all-to-all-start.6 = ((bf16[4,192,768]{2,1,0:T(8,128)(2,1)}), bf16[4,192,768]{2,1,0:T(8,128)(2,1)S(1)}, u32[]{:S(2)}, u32[]{:S(2)}) async-start(bf16[4,192,768]{2,1,0:T(8,128)(2,1)} %bitcast.13), calls=%async_computation.6 | async-start | bytes 2359296 | tf_op jit(solution)/shard_map/all_to_all | solution.py:25
  187.6 14.8 %all-to-all-done.6 = bf16[4,192,768]{2,1,0:T(8,128)(2,1)S(1)} async-done(((bf16[4,192,768]{2,1,0:T(8,128)(2,1)}), bf16[4,192,768]{2,1,0:T(8,128)(2,1)S(1)}, u32[]{:S(2)}, u32[]{:S(2)}) %all-to-all-start.6) | async-done | bytes 1179680 | tf_op jit(solution)/shard_map/all_to_all | solution.py:25
  202.7 18.4 %all_to_all.48 = bf16[4,192,768]{2,1,0:T(8,128)(2,1)S(1)} all-to-all(bf16[4,192,768]{2,1,0:T(8,128)(2,1)S(1)} %broadcast_in_dim.20), channel_id=1, replica_groups=mesh['y'=4,'core'=2,'z'=8,'x'=4] {'y'}, dimensions={0} | all-to-all | bytes 2359296 | tf_op jit(solution)/shard_map/all_to_all | solution.py:16
  221.1 1.6 broadcast_in_dim.21
  222.7 3.8 %all-to-all-start.8 = ((bf16[2,768,768]{2,1,0:T(8,128)(2,1)}), bf16[2,768,768]{2,1,0:T(8,128)(2,1)S(1)}, u32[]{:S(2)}, u32[]{:S(2)}) async-start(bf16[2,768,768]{2,1,0:T(8,128)(2,1)} %broadcast_in_dim.21), calls=%async_computation.8 | async-start | bytes 4718592 | tf_op jit(solution)/shard_map/all_to_all | solution.py:16
  226.6 3.0 %all-to-all-done.8 = bf16[2,768,768]{2,1,0:T(8,128)(2,1)S(1)} async-done(((bf16[2,768,768]{2,1,0:T(8,128)(2,1)}), bf16[2,768,768]{2,1,0:T(8,128)(2,1)S(1)}, u32[]{:S(2)}, u32[]{:S(2)}) %all-to-all-start.8) | async-done | bytes 2359328 | tf_op jit(solution)/shard_map/all_to_all | solution.py:16
  229.5 4.7 %convolution_convert_fusion = bf16[1536,768]{1,0:T(8,128)(2,1)} fusion(bf16[1536,768]{1,0:T(8,128)(2,1)S(1)} %bitcast.42, bf16[768,768]{0,1:T(8,128)(2,1)} %all-gather.8.cloned.1.call-done), kind=kOutput, calls=%fused_computation | convolution fusion | flops 1813118976 | bytes 5898240 | tf_op jit(solution)/shard_map/dot_general | solution.py:11
  234.3 41.1 %reduce-scatter.5.cloned.1.call-done = bf16[192,768]{1,0:T(8,128)(2,1)} async-done(((bf16[1536,768]{1,0:T(8,128)(2,1)}), bf16[192,768]{1,0:T(8,128)(2,1)}) %reduce-scatter.5.cloned.1.call-update) | async-done | bytes 294928 | tf_op jit(solution)/shard_map/reduce_scatter | solution.py:51
  (28 shorter events, 4.0 us)
Async XLA Ops:
  6.5 7.5 %copy-start = (bf16[768,192]{0,1:T(8,128)(2,1)S(1)}, bf16[768,192]{0,1:T(8,128)(2,1)}, u32[]{:S(2)}) copy-start(bf16[768,192]{0,1:T(8,128)(2,1)} %param.7) | copy-start | bytes 884740
  6.5 60.2 %all-gather.4.cloned.1.call-start = ((), (), s32[]{:S(2)}) async-start(), calls=%async_computation.11 | async-start | bytes 2654208 | tf_op jit(solution)/shard_map/all_gather | solution.py:31
  9.3 10.8 %all-to-all-start = ((bf16[4,192,192]{1,2,0:T(8,128)(2,1)}), bf16[4,192,192]{1,2,0:T(8,128)(2,1)S(1)}, u32[]{:S(2)}, u32[]{:S(2)}) async-start(bf16[4,192,192]{1,2,0:T(8,128)(2,1)} %pad_maximum_fusion), calls=%async_computation | async-start | bytes 786432 | tf_op jit(solution)/shard_map/all_to_all | solution.py:33
  14.1 32.1 %collective-permute-start = (bf16[768,192]{0,1:T(8,128)(2,1)S(1)}, bf16[768,192]{0,1:T(8,128)(2,1)S(1)}, u32[]{:S(2)}, u32[]{:S(2)}) collective-permute-start(bf16[768,192]{0,1:T(8,128)(2,1)S(1)} %copy-done), channel_id=1, source_target_pairs={{0,0},{4,32},{8,64},{12,96},{16,128},{20,160},{24,192},{28,224},{3... | collective-permute-start | bytes 884744 | tf_op jit(solution)/shard_map/ppermute | solution.py:36
  21.8 36.3 %all-to-all-start.1 = ((bf16[8,192,768]{2,1,0:T(8,128)(2,1)}), bf16[8,192,768]{2,1,0:T(8,128)(2,1)S(1)}, u32[]{:S(2)}, u32[]{:S(2)}) async-start(bf16[8,192,768]{2,1,0:T(8,128)(2,1)} %broadcast_in_dim.17), calls=%async_computation.1 | async-start | bytes 4718592 | tf_op jit(solution)/shard_map/all_to_all | solution.py:16
  29.6 65.5 %all-gather.6.cloned.1.call-start = ((), (), s32[]{:S(2)}) async-start(), calls=%async_computation.12 | async-start | bytes 2654208 | tf_op jit(solution)/shard_map/all_gather | solution.py:37
  46.2 0.7 copy-start.1
  88.5 16.8 %all-to-all-start.3 = ((bf16[4,192,768]{2,1,0:T(8,128)(2,1)}), bf16[4,192,768]{2,1,0:T(8,128)(2,1)S(1)}, u32[]{:S(2)}, u32[]{:S(2)}) async-start(bf16[4,192,768]{2,1,0:T(8,128)(2,1)} %broadcast_in_dim.18), calls=%async_computation.3 | async-start | bytes 2359296 | tf_op jit(solution)/shard_map/all_to_all | solution.py:16
  94.1 61.8 %reduce-scatter.7.cloned.1.call-start = ((), (), s32[]{:S(2)}) async-start(), calls=%async_computation.15 | async-start | bytes 2654208
  111.5 44.4 %copy-start.2 = (f32[768]{0:T(1024)S(1)}, f32[768]{0:T(1024)}, u32[]{:S(2)}) copy-start(f32[768]{0:T(1024)} %param.8) | copy-start | bytes 9220
  111.5 44.4 %copy-start.3 = (f32[192]{0:T(256)S(1)}, f32[192]{0:T(256)}, u32[]{:S(2)}) copy-start(f32[192]{0:T(256)} %param.9) | copy-start | bytes 2308
  111.5 59.9 %copy-start.4 = (bf16[1536,768]{1,0:T(8,128)(2,1)S(1)}, bf16[1536,768]{1,0:T(8,128)(2,1)}, u32[]{:S(2)}) copy-start(bf16[1536,768]{1,0:T(8,128)(2,1)} %all-gather.4.cloned.1.call-done) | copy-start | bytes 7077892
  181.9 20.5 %all-to-all-start.6 = ((bf16[4,192,768]{2,1,0:T(8,128)(2,1)}), bf16[4,192,768]{2,1,0:T(8,128)(2,1)S(1)}, u32[]{:S(2)}, u32[]{:S(2)}) async-start(bf16[4,192,768]{2,1,0:T(8,128)(2,1)} %bitcast.13), calls=%async_computation.6 | async-start | bytes 2359296 | tf_op jit(solution)/shard_map/all_to_all | solution.py:25
  187.0 39.5 %all-gather.8.cloned.1.call-start = ((), (), s32[]{:S(2)}) async-start(), calls=%async_computation.13 | async-start | bytes 1474560 | tf_op jit(solution)/shard_map/all_gather | solution.py:44
  222.7 6.9 %all-to-all-start.8 = ((bf16[2,768,768]{2,1,0:T(8,128)(2,1)}), bf16[2,768,768]{2,1,0:T(8,128)(2,1)S(1)}, u32[]{:S(2)}, u32[]{:S(2)}) async-start(bf16[2,768,768]{2,1,0:T(8,128)(2,1)} %broadcast_in_dim.21), calls=%async_computation.8 | async-start | bytes 4718592 | tf_op jit(solution)/shard_map/all_to_all | solution.py:16
  226.5 48.9 %reduce-scatter.5.cloned.1.call-start = ((), (), s32[]{:S(2)}) async-start(), calls=%async_computation.14 | async-start | bytes 2654208 | tf_op jit(solution)/shard_map/reduce_scatter | solution.py:51
Sparse Core Ops, SparseCore 0:
  9.1 57.5 all-gather.3
  68.5 26.5 all-gather.5
  111.6 44.2 reduce-scatter.6
  189.3 24.6 all-gather.7
  234.4 40.9 reduce-scatter.4
